TPU v7x, 512 devices: a 4x2x32 block of a 4x16x32 slice. The times are simulated.
512 devices in a mesh: group: 2 (over y), expert: 32 (over z), tensor: 4 (over x), sub: 2 (over core).
Axes of the slice: x: 4, y: 2, z: 32, core: 2. Of those that a mesh axis runs over, the one named last changes fastest.
The devices are a block of a 4x16x32 slice.
Arguments:
- tokens: bfloat16 [512, 7168], P(('group', 'expert', 'sub')), parts along dimension 0, may hold values from -6 to 6
- expert_ids: int32 [512, 8], P(('group', 'expert', 'sub')), parts along dimension 0, may hold values from 0 to 15, all different within a row; in each aligned block of 4 rows (0 to 3, 4 to 7, ...) at most 3 rows name the same one
- gate_codes: int32 [512, 8], P(('group', 'expert', 'sub')), parts along dimension 0, may hold values from 1 to 63
- w_gate: bfloat16 [32, 1024, 7168], P('expert', ('tensor', 'sub')), may hold values from -0.0625 to 0.0625
- w_up: bfloat16 [32, 1024, 7168], P('expert', ('tensor', 'sub')), may hold values from -0.0625 to 0.0625
- w_down: bfloat16 [32, 1024, 7168], P('expert', ('tensor', 'sub')), may hold values from -0.125 to 0.125
Outputs:
- mixed: bfloat16 [512, 7168], P(('group', 'expert', 'sub'), 'tensor'), parts along dimension 0
There are 2 independent parts, one for each index of `group`. A program takes and returns all parts, laid end to end along the dimension named above; an argument that names none is the same for every part. Nothing has to cross between parts.
Inputs may be any that keep to these rules, and one draw needn't show every extreme that they name: `expert_ids`: the 8 numbers of a row differ; within the rows of one device (aligned blocks of 4 rows) no expert is named by more than 3 rows, a bound that some block reaches.
All inputs are finite; a program needn't handle non-finite values.
Results may differ from a plain program's by a relative error of at most 0.008.
Values may be sent and summed in bfloat16 or wider, within the bound.
A program may use at most 64 MiB of HBM per device.

v0:
```python
import jax
import jax.numpy as jnp
from jax import lax
from jax.sharding import PartitionSpec as P


def shards(tokens, expert_ids, gate_codes, w_gate, w_up, w_down):
    tok_rows, features = tokens.shape
    per_token = expert_ids.shape[1]
    owners = lax.axis_size("expert")
    sub_count = lax.axis_size("sub")
    tensor_count = lax.axis_size("tensor")
    experts = owners // 2
    capacity = min(tok_rows, tok_rows * per_token // experts + 1)
    flat_ids = expert_ids.reshape(-1)
    matches = (flat_ids[:, None] == jnp.arange(experts, dtype=jnp.int32)[None, :]).astype(jnp.int32)
    before = jnp.cumsum(matches, axis=0) - matches
    slot_index = jnp.sum(before * matches, axis=1)
    position = flat_ids * capacity + slot_index
    onehot = position[:, None] == jnp.arange(experts * capacity, dtype=jnp.int32)[None, :]
    weights = gate_codes.reshape(-1).astype(jnp.float32) / 64.0
    choose = jnp.any(onehot.reshape(tok_rows, per_token, -1), axis=1).astype(jnp.bfloat16)
    combine = jnp.sum(
        jnp.where(onehot, weights[:, None], 0.0).reshape(tok_rows, per_token, -1), axis=1
    )
    packed = jnp.dot(choose.T, tokens, preferred_element_type=jnp.float32).astype(jnp.bfloat16)
    outgoing = jnp.broadcast_to(
        packed.reshape(experts, 1, capacity, features), (experts, 2, capacity, features)
    )
    arrived = lax.all_to_all(
        outgoing.reshape(owners, capacity, features),
        "expert",
        split_axis=0,
        concat_axis=0,
        tiled=True,
    )
    slot_rows = lax.all_gather(arrived, "sub", axis=1, tiled=True).reshape(-1, features)
    contract = (((1,), (1,)), ((), ()))
    gate_act = lax.dot_general(slot_rows, w_gate[0], contract, preferred_element_type=jnp.float32)
    up_act = lax.dot_general(slot_rows, w_up[0], contract, preferred_element_type=jnp.float32)
    hidden = (jax.nn.silu(gate_act) * up_act).astype(jnp.bfloat16)
    partial_value = jnp.dot(hidden, w_down[0], preferred_element_type=jnp.float32).astype(
        jnp.bfloat16
    )
    partial_value = partial_value.reshape(owners, sub_count, capacity, features)
    block = features // tensor_count
    sectioned = partial_value.reshape(owners, sub_count, capacity, tensor_count, block).transpose(
        0, 2, 3, 1, 4
    )
    sectioned = sectioned.reshape(owners, capacity, tensor_count * sub_count, block)
    gathered = lax.all_to_all(sectioned, ("tensor", "sub"), split_axis=2, concat_axis=2, tiled=True)
    run_total = jnp.sum(gathered.astype(jnp.float32), axis=2)
    came_back = lax.all_to_all(
        run_total.astype(jnp.bfloat16), "expert", split_axis=0, concat_axis=0, tiled=True
    ).astype(run_total.dtype)
    summed = jnp.sum(came_back.reshape(experts, 2, capacity, block), axis=1)
    mixed = jnp.dot(
        combine,
        summed.reshape(-1, block),
        precision=lax.Precision.HIGHEST,
        preferred_element_type=jnp.float32,
    )
    return mixed.astype(jnp.bfloat16)


def solution(mesh):
    return jax.shard_map(
        shards,
        mesh=mesh,
        in_specs=(
            P(("group", "expert", "sub"), None),
            P(("group", "expert", "sub"), None),
            P(("group", "expert", "sub"), None),
            P("expert", ("tensor", "sub"), None),
            P("expert", ("tensor", "sub"), None),
            P("expert", ("tensor", "sub"), None),
        ),
        out_specs=P(("group", "expert", "sub"), "tensor"),
        check_vma=False,
    )
```

profile of v0, /device:TPU:40, one launch (start us, length us, event | category | flops | bytes accessed | tf_op | source)
XLA Modules:
  0.0 407.4 jit_solution(4467936220724837105)
XLA Ops:
  6.5 0.0 copy-start
  6.6 0.0 all-gather.2.cloned.1.call-start
  6.6 0.9 eq.30
  7.4 0.1 fusion.20
  7.5 0.1 reduce_window_sum.11
  7.6 0.2 select_reduce_fusion.1
  7.8 0.1 reduce_sum.42
  7.8 0.7 multiply_add_fusion
  8.5 0.1 fusion.19
  8.6 1.2 convolution_convert_fusion.1
  9.8 0.4 broadcast_in_dim.25
  10.3 0.5 broadcast_in_dim.26
  10.8 221.8 %all_to_all.15 = bf16[32,3,7168]{2,1,0:T(4,128)(2,1)S(1)} all-to-all(bf16[32,3,7168]{2,1,0:T(4,128)(2,1)S(1)} %bitcast.29), channel_id=1, replica_groups=mesh['group'=2,'expert'=32,'tensor'=4,'sub'=2] {'expert'}, dimensions={0} | all-to-all | bytes 2752512 | tf_op jit(solution)/shard_map/all_to_all | solution.py:30
  232.6 1.6 copy.21
  234.2 0.1 all-gather.2.cloned.1.call-update
  234.3 12.8 %all-gather.2.cloned.1.call-done = bf16[32,6,7168]{2,0,1:T(8,128)(2,1)} async-done(((bf16[32,3,7168]{2,0,1:T(8,128)(2,1)}), bf16[32,6,7168]{2,0,1:T(8,128)(2,1)}) %all-gather.2.cloned.1.call-update) | async-done | bytes 2752528 | tf_op jit(solution)/shard_map/all_gather | solution.py:37
  247.1 5.1 %copy.22 = bf16[32,6,7168]{2,1,0:T(8,128)(2,1)} copy(bf16[32,6,7168]{2,0,1:T(8,128)(2,1)} %all-gather.2.cloned.1.call-done) | data formatting | bytes 5505024 | tf_op jit(solution)/shard_map/all_gather | solution.py:37
  252.2 4.6 %reshape.60 = bf16[192,7168]{1,0:T(8,128)(2,1)} reshape(bf16[32,6,7168]{2,1,0:T(8,128)(2,1)} %copy.22) | data formatting | bytes 5505024 | tf_op jit(solution)/shard_map/reshape | solution.py:37
  256.9 3.2 fusion.3
  260.1 0.0 copy-done
  260.1 7.0 %convolution_convert_fusion = bf16[192,7168]{1,0:T(8,128)(2,1)} fusion(bf16[1,128,7168]{2,1,0:T(8,128)(2,1)S(1)} %copy-done, bf16[192,7168]{1,0:T(8,128)(2,1)} %reshape.60, bf16[1,128,7168]{2,1,0:T(8,128)(2,1)} %param.10, f32[192,128]{1,0:T(8,128)S(1)} %fusion.3), kind=kOutput, calls=%fused_computation | convolution fusion | flops 706166784 | bytes 9273344 | tf_op jit(solution)/shard_map/dot_general | solution.py:42
  267.0 6.2 %reshape_reshape.3 = bf16[32,2,3,4,1792]{4,3,2,1,0:T(4,128)(2,1)} reshape(bf16[192,7168]{1,0:T(8,128)(2,1)} %convolution_convert_fusion) | data formatting | bytes 5505024 | tf_op jit(solution)/shard_map/reshape;reshape | solution.py:47
  273.3 2.3 copy.29
  275.6 38.4 %all_to_all.16 = bf16[32,3,8,1792]{3,0,1,2:T(8,128)(2,1)} all-to-all(bf16[32,3,8,1792]{3,0,1,2:T(8,128)(2,1)S(1)} %bitcast.28), channel_id=1, replica_groups=mesh['group'=2,'expert'=32,'tensor'=4,'sub'=2] {'tensor','sub'}, dimensions={2} | all-to-all | bytes 5505024 | tf_op jit(solution)/shard_map/all_to_all | solution.py:51
  314.0 0.0 copy-start.1
  314.0 2.2 reduce_sum.44
  316.2 1.1 copy.26
  317.3 23.3 %all-to-all-start.2 = ((bf16[32,3,1792]{2,1,0:T(4,128)(2,1)}), bf16[32,3,1792]{2,1,0:T(4,128)(2,1)S(1)}, u32[]{:S(2)}, u32[]{:S(2)}) async-start(bf16[32,3,1792]{2,1,0:T(4,128)(2,1)} %copy.26), calls=%async_computation.2 | async-start | bytes 917504 | tf_op jit(solution)/shard_map/all_to_all | solution.py:53
  340.6 0.0 copy-done.1
  340.7 0.1 select_reduce_fusion
  340.7 58.5 %all-to-all-done.2 = bf16[32,3,1792]{2,1,0:T(4,128)(2,1)S(1)} async-done(((bf16[32,3,1792]{2,1,0:T(4,128)(2,1)}), bf16[32,3,1792]{2,1,0:T(4,128)(2,1)S(1)}, u32[]{:S(2)}, u32[]{:S(2)}) %all-to-all-start.2) | async-done | bytes 344096 | tf_op jit(solution)/shard_map/all_to_all | solution.py:53
  399.2 0.3 convert_reduce_fusion
  399.5 0.2 reshape.64
  399.6 0.9 convolution_convert_fusion.2
  (1 shorter events, 0.0 us)
Async XLA Ops:
  6.5 253.5 %copy-start = (bf16[1,128,7168]{2,1,0:T(8,128)(2,1)S(1)}, bf16[1,128,7168]{2,1,0:T(8,128)(2,1)}, u32[]{:S(2)}) copy-start(bf16[1,128,7168]{2,1,0:T(8,128)(2,1)} %param.11) | copy-start | bytes 5505028
  6.6 240.6 %all-gather.2.cloned.1.call-start = ((), (), s32[]{:S(2)}) async-start(), calls=%async_computation.3 | async-start | bytes 4128768 | tf_op jit(solution)/shard_map/all_gather | solution.py:37
  314.0 26.6 %copy-start.1 = (s32[4,8]{1,0:T(4,128)S(1)}, s32[4,8]{1,0:T(4,128)}, u32[]{:S(2)}) copy-start(s32[4,8]{1,0:T(4,128)} %param.8) | copy-start | bytes 388
  317.3 81.9 %all-to-all-start.2 = ((bf16[32,3,1792]{2,1,0:T(4,128)(2,1)}), bf16[32,3,1792]{2,1,0:T(4,128)(2,1)S(1)}, u32[]{:S(2)}, u32[]{:S(2)}) async-start(bf16[32,3,1792]{2,1,0:T(4,128)(2,1)} %copy.26), calls=%async_computation.2 | async-start | bytes 917504 | tf_op jit(solution)/shard_map/all_to_all | solution.py:53
Sparse Core Ops, SparseCore 0:
  234.4 12.6 all-gather.1
where the time goes:
time: 408 us; the launch traced here: 407 us
  blocking collectives  260 us (64%)
  waiting for transfers between devices  71.3 us (17%)
  starting transfers between devices  23.3 us (6%)
  local copies, waits for them, and re-layouts  23.1 us (6%)
  between operations  13.5 us (3%)
  matrix products  12.2 us (3%)
    all_to_all x1, blocking collectives, shards(): lax.all_to_all(outgoing.reshape(owners, capacity, features), 'expert', sp...  222 us
    all_to_all x1, waiting for transfers between devices, shards(): lax.all_to_all(run_total.astype(jnp.bfloat16), 'expert', split_axis=0, co...  58.5 us
    all_to_all x1, blocking collectives, shards(): lax.all_to_all(sectioned, ('tensor', 'sub'), split_axis=2, concat_axis=2,...  38.4 us
    all_to_all x1, starting transfers between devices, shards(): lax.all_to_all(run_total.astype(jnp.bfloat16), 'expert', split_axis=0, co...  23.3 us
    all_gather x1, waiting for transfers between devices, shards(): lax.all_gather(arrived, 'sub', axis=1, tiled=True).reshape(-1, features)  12.8 us
  transfers between devices with their start and end apart: 2, of which 2 were waited for; matrix products, arithmetic and copies ran while one was open for 0% of the time, Pallas kernels for 0%

commit v1 on v0

--- a/solution.py
+++ b/solution.py
@@ -34,7 +34,9 @@
         concat_axis=0,
         tiled=True,
     )
-    slot_rows = lax.all_gather(arrived, "sub", axis=1, tiled=True).reshape(-1, features)
+    slot_rows = jnp.concatenate(
+        jax.lax.all_to_all(jnp.stack(jax.lax.psum(1, "sub") * [arrived]), "sub", 0, 0), axis=1
+    ).reshape(-1, features)
     contract = (((1,), (1,)), ((), ()))
     gate_act = lax.dot_general(slot_rows, w_gate[0], contract, preferred_element_type=jnp.float32)
     up_act = lax.dot_general(slot_rows, w_up[0], contract, preferred_element_type=jnp.float32)

time: 408 us -> 373 us (0.914)
  starting transfers between devices: 23.3 us -> 4.8 us
  between operations: 13.5 us -> 0.1 us
  waiting for transfers between devices: 71.3 us -> 58.8 us
  blocking collectives: 260 us -> 266 us
    all_to_all x1, starting transfers between devices: 23.3 us -> 4.8 us  [shards(): lax.all_to_all(run_total.astype(jnp.bfloat16), 'expert', split_axis=0, co...]
    all_gather x1 -> x0, waiting for transfers between devices: 12.8 us -> none  [shards(): lax.all_gather(arrived, 'sub', axis=1, tiled=True).reshape(-1, features)]
    another operation x0 -> x2, local copies, waits for them, and re-layouts: none -> 8.13 us  [the longest x1 7.07 us: shards(): slot_rows = jnp.concatenate(jax.lax.all_to_all(jnp.stack(jax.lax.psum(1,...]
    all_to_all x0 -> x1, blocking collectives: none -> 5.96 us  [shards(): jax.lax.all_to_all(jnp.stack(jax.lax.psum(1, 'sub') * [arrived]), 'sub',...]
    all_gather x1 -> x0, local copies, waits for them, and re-layouts: 5.11 us -> none  [shards(): lax.all_gather(arrived, 'sub', axis=1, tiled=True).reshape(-1, features)]
  transfers between devices with their start and end apart: 2 -> 1, of which waited for: 2 -> 1; matrix products, arithmetic and copies ran while one was open for 0% -> 0% of each run, Pallas kernels for 0% -> 0%
where the time goes in v1:
time: 373 us; the launch traced here: 372 us
  blocking collectives  266 us (71%)
  waiting for transfers between devices  58.8 us (16%)
  local copies, waits for them, and re-layouts  24 us (6%)
  matrix products  12.2 us (3%)
  other arithmetic  5.34 us (1%)
  starting transfers between devices  4.8 us (1%)
    all_to_all x1, blocking collectives, shards(): lax.all_to_all(outgoing.reshape(owners, capacity, features), 'expert', sp...  222 us
    all_to_all x1, waiting for transfers between devices, shards(): lax.all_to_all(run_total.astype(jnp.bfloat16), 'expert', split_axis=0, co...  58.8 us
    all_to_all x1, blocking collectives, shards(): lax.all_to_all(sectioned, ('tensor', 'sub'), split_axis=2, concat_axis=2,...  38.7 us
  transfers between devices with their start and end apart: 1, of which 1 were waited for; matrix products, arithmetic and copies ran while one was open for 0% of the time, Pallas kernels for 0%

profile of v1, /device:TPU:40, one launch (start us, length us, event | category | flops | bytes accessed | tf_op | source)
XLA Modules:
  0.0 371.8 jit_solution(7873419184703963555)
XLA Ops:
  0.0 0.0 copy-start
  0.0 0.9 eq.30
  0.9 0.1 fusion.20
  1.0 0.1 reduce_window_sum.11
  1.0 0.2 select_reduce_fusion.1
  1.2 0.1 reduce_sum.42
  1.3 0.7 multiply_add_fusion
  2.0 0.1 fusion.19
  2.1 1.2 convolution_convert_fusion.1
  3.3 0.4 broadcast_in_dim.25
  3.8 0.5 broadcast_in_dim.26
  4.3 221.8 %all_to_all.20 = bf16[32,3,7168]{2,1,0:T(4,128)(2,1)S(1)} all-to-all(bf16[32,3,7168]{2,1,0:T(4,128)(2,1)S(1)} %bitcast.32), channel_id=1, replica_groups=mesh['group'=2,'expert'=32,'tensor'=4,'sub'=2] {'expert'}, dimensions={0} | all-to-all | bytes 2752512 | tf_op jit(solution)/shard_map/all_to_all | solution.py:30
  226.1 1.7 pad_maximum_fusion
  227.8 1.1 copy.21
  228.8 6.0 %all_to_all.21 = bf16[2,32,3,7168]{3,1,2,0:T(8,128)(2,1)S(1)} all-to-all(bf16[2,32,3,7168]{3,1,2,0:T(8,128)(2,1)S(1)} %copy.21), channel_id=1, replica_groups=mesh['group'=2,'expert'=32,'tensor'=4,'sub'=2] {'sub'}, dimensions={0} | all-to-all | bytes 5505024 | tf_op jit(solution)/shard_map/all_to_all | solution.py:38
  234.8 4.2 %copy.22 = bf16[32,2,3,7168]{3,2,1,0:T(4,128)(2,1)} copy(bf16[32,2,3,7168]{3,0,2,1:T(8,128)(2,1)S(1)} %bitcast.30) | data formatting | bytes 5505024 | tf_op jit(solution)/shard_map/reshape | solution.py:37
  238.9 7.1 %reshape_reshape.6 = bf16[192,7168]{1,0:T(8,128)(2,1)} reshape(bf16[32,2,3,7168]{3,2,1,0:T(4,128)(2,1)} %copy.22) | data formatting | bytes 5505024 | tf_op jit(solution)/shard_map/reshape;reshape | solution.py:39
  246.0 3.2 fusion.3
  249.2 0.0 copy-done
  249.2 7.0 %convolution_convert_fusion = bf16[192,7168]{1,0:T(8,128)(2,1)} fusion(bf16[1,128,7168]{2,1,0:T(8,128)(2,1)S(1)} %copy-done, bf16[192,7168]{1,0:T(8,128)(2,1)} %reshape_reshape.6, bf16[1,128,7168]{2,1,0:T(8,128)(2,1)} %param.10, f32[192,128]{1,0:T(8,128)S(1)} %fusion.3), kind=kOutput, calls=%fused_computation | convolution fusion | flops 706166784 | bytes 9273344 | tf_op jit(solution)/shard_map/dot_general | solution.py:44
  256.2 6.2 %reshape_reshape.7 = bf16[32,2,3,4,1792]{4,3,2,1,0:T(4,128)(2,1)} reshape(bf16[192,7168]{1,0:T(8,128)(2,1)} %convolution_convert_fusion) | data formatting | bytes 5505024 | tf_op jit(solution)/shard_map/reshape;reshape | solution.py:49
  262.4 2.3 copy.29
  264.7 38.7 %all_to_all.22 = bf16[32,3,8,1792]{3,0,1,2:T(8,128)(2,1)} all-to-all(bf16[32,3,8,1792]{3,0,1,2:T(8,128)(2,1)S(1)} %bitcast.31), channel_id=1, replica_groups=mesh['group'=2,'expert'=32,'tensor'=4,'sub'=2] {'tensor','sub'}, dimensions={2} | all-to-all | bytes 5505024 | tf_op jit(solution)/shard_map/all_to_all | solution.py:53
  303.5 0.0 copy-start.1
  303.5 2.2 reduce_sum.44
  305.7 1.1 copy.26
  306.8 4.8 %all-to-all-start.3 = ((bf16[32,3,1792]{2,1,0:T(4,128)(2,1)}), bf16[32,3,1792]{2,1,0:T(4,128)(2,1)S(1)}, u32[]{:S(2)}, u32[]{:S(2)}) async-start(bf16[32,3,1792]{2,1,0:T(4,128)(2,1)} %copy.26), calls=%async_computation.3 | async-start | bytes 917504 | tf_op jit(solution)/shard_map/all_to_all | solution.py:55
  311.6 0.0 copy-done.1
  311.6 0.1 select_reduce_fusion
  311.7 58.8 %all-to-all-done.3 = bf16[32,3,1792]{2,1,0:T(4,128)(2,1)S(1)} async-done(((bf16[32,3,1792]{2,1,0:T(4,128)(2,1)}), bf16[32,3,1792]{2,1,0:T(4,128)(2,1)S(1)}, u32[]{:S(2)}, u32[]{:S(2)}) %all-to-all-start.3) | async-done | bytes 344096 | tf_op jit(solution)/shard_map/all_to_all | solution.py:55
  370.5 0.3 convert_reduce_fusion
  370.8 0.2 reshape.64
  370.9 0.9 convolution_convert_fusion.2
  (1 shorter events, 0.0 us)
Async XLA Ops:
  0.0 249.2 %copy-start = (bf16[1,128,7168]{2,1,0:T(8,128)(2,1)S(1)}, bf16[1,128,7168]{2,1,0:T(8,128)(2,1)}, u32[]{:S(2)}) copy-start(bf16[1,128,7168]{2,1,0:T(8,128)(2,1)} %param.11) | copy-start | bytes 5505028
  303.5 8.1 %copy-start.1 = (s32[4,8]{1,0:T(4,128)S(1)}, s32[4,8]{1,0:T(4,128)}, u32[]{:S(2)}) copy-start(s32[4,8]{1,0:T(4,128)} %param.8) | copy-start | bytes 388
  306.8 63.7 %all-to-all-start.3 = ((bf16[32,3,1792]{2,1,0:T(4,128)(2,1)}), bf16[32,3,1792]{2,1,0:T(4,128)(2,1)S(1)}, u32[]{:S(2)}, u32[]{:S(2)}) async-start(bf16[32,3,1792]{2,1,0:T(4,128)(2,1)} %copy.26), calls=%async_computation.3 | async-start | bytes 917504 | tf_op jit(solution)/shard_map/all_to_all | solution.py:55
